TPU v7x, 128 devices: a whole 4x4x4 slice. The times are simulated.
128 devices in a mesh: bank: 4 (over y_lo, core), zero: 32 (over z, y_hi, x).
Axes of the slice: x: 4, y: 4 (y_hi: 2, y_lo: 2; y = y_hi * 2 + y_lo), z: 4, core: 2. Of those that a mesh axis runs over, the one named last changes fastest.
Arguments:
- train_gate: float32 [128, 2048, 768], P('bank', 'zero'), may hold values from -0.25 to 0.25
- other_gate: bfloat16 [128, 2048, 768], P('bank', 'zero'), may hold values from -0.0625 to 0.0625
- train_up: float32 [128, 2048, 768], P('bank', 'zero'), may hold values from -0.25 to 0.25
- other_up: bfloat16 [128, 2048, 768], P('bank', 'zero'), may hold values from -0.0625 to 0.0625
- router_weight: float32 [2048, 128], P('zero', 'bank'), may hold values from -0.125 to 0.125
- router_gain: float32 [2048], P('zero'), may hold values from 0.25 to 1.75
Outputs:
- ready_gate: bfloat16 [128, 2048, 768], P(('bank', 'zero'))
- ready_up: bfloat16 [128, 2048, 768], P(('bank', 'zero'))
- scale_gate: float32 [128, 768], P(('bank', 'zero'))
- scale_up: float32 [128, 768], P(('bank', 'zero'))
- serve_router: bfloat16 [2048, 128], replicated
All inputs are finite; a program needn't handle non-finite values.
Results may differ from a plain program's by a relative error of at most 0.0075.
Values may be sent and summed in bfloat16 or wider, within the bound.
No kernel may reach another device: no remote copies, remote signals or barrier semaphores. Data moves between devices by JAX's collectives and lax.ppermute only.
A program may use at most 128 MiB of HBM per device.

v0:
```python
import jax
import jax.numpy as jnp
from jax import lax
from jax.sharding import PartitionSpec as P


def regrouped(train, other):
    latest = (train + other.astype(jnp.float32)).astype(jnp.bfloat16)
    return lax.all_to_all(latest, "zero", split_axis=0, concat_axis=1, tiled=True)


def normalised(pieces):
    wide = pieces.astype(jnp.float32)
    scale = jnp.sqrt(jnp.sum(wide * wide, axis=1))
    return ((wide / scale[:, None, :]).astype(jnp.bfloat16), scale)


def body(train_gate, other_gate, train_up, other_up, router_weight, router_gain):
    gate = regrouped(train_gate, other_gate)
    up = regrouped(train_up, other_up)
    part_router = (router_weight * router_gain[:, None]).astype(jnp.bfloat16)
    serve_router = lax.all_gather(part_router, "zero", axis=0, tiled=True)
    serve_router = lax.all_gather(serve_router, "bank", axis=1, tiled=True)
    ready_gate, scale_gate = normalised(gate)
    ready_up, scale_up = normalised(up)
    return (ready_gate, ready_up, scale_gate, scale_up, serve_router)


def solution(mesh):
    placed = (
        P("bank", "zero", None),
        P("bank", "zero", None),
        P("bank", "zero", None),
        P("bank", "zero", None),
        P("zero", "bank"),
        P("zero"),
    )
    return jax.shard_map(
        body,
        mesh=mesh,
        in_specs=placed,
        out_specs=(
            P(("bank", "zero"), None, None),
            P(("bank", "zero"), None, None),
            P(("bank", "zero"), None),
            P(("bank", "zero"), None),
            P(),
        ),
        check_vma=False,
    )
```

profile of v0, /device:TPU:1, one launch (start us, length us, event | category | flops | bytes accessed | tf_op | source)
XLA Modules:
  0.0 215.3 jit_solution(7930058115264093325)
XLA Ops:
  0.6 6.4 %add_convert_fusion = bf16[32,64,768]{2,1,0:T(8,128)(2,1)} fusion(f32[32,64,768]{2,1,0:T(8,128)} %param.8, bf16[32,64,768]{2,1,0:T(8,128)(2,1)} %param.9), kind=kLoop, calls=%fused_computation.5 | loop fusion | flops 4718592 | bytes 12582912 | tf_op jit(solution)/shard_map/convert_element_type | solution.py:8
  7.0 11.3 %all-to-all-start.1 = ((bf16[32,64,768]{2,1,0:T(8,128)(2,1)}), bf16[32,64,768]{2,1,0:T(8,128)(2,1)S(1)}, u32[]{:S(2)}, u32[]{:S(2)}) async-start(bf16[32,64,768]{2,1,0:T(8,128)(2,1)} %add_convert_fusion), calls=%async_computation.1 | async-start | bytes 6291456 | tf_op jit(solution)/shard_map/all_to_all | solution.py:9
  18.4 6.4 %add_convert_fusion.1 = bf16[32,64,768]{2,1,0:T(8,128)(2,1)} fusion(f32[32,64,768]{2,1,0:T(8,128)} %param.6, bf16[32,64,768]{2,1,0:T(8,128)(2,1)} %param.7), kind=kLoop, calls=%fused_computation.7 | loop fusion | flops 4718592 | bytes 12582912 | tf_op jit(solution)/shard_map/convert_element_type | solution.py:8
  24.8 0.0 copy-start.1
  24.8 0.0 copy-start.2
  24.8 34.0 %all-to-all-done.1 = bf16[32,64,768]{2,1,0:T(8,128)(2,1)S(1)} async-done(((bf16[32,64,768]{2,1,0:T(8,128)(2,1)}), bf16[32,64,768]{2,1,0:T(8,128)(2,1)S(1)}, u32[]{:S(2)}, u32[]{:S(2)}) %all-to-all-start.1) | async-done | bytes 3145760 | tf_op jit(solution)/shard_map/all_to_all | solution.py:9
  58.8 0.0 copy-start
  58.8 1.7 copy-done
  60.5 9.2 %all-to-all-start = ((bf16[32,64,768]{2,1,0:T(8,128)(2,1)}), bf16[32,64,768]{2,1,0:T(8,128)(2,1)S(1)}, u32[]{:S(2)}, u32[]{:S(2)}) async-start(bf16[32,64,768]{2,1,0:T(8,128)(2,1)} %add_convert_fusion.1), calls=%async_computation | async-start | bytes 6291456 | tf_op jit(solution)/shard_map/all_to_all | solution.py:9
  69.6 0.0 copy-done.1
  69.6 0.0 copy-done.2
  69.7 109.4 %all-gather = bf16[32,64,32]{1,2,0:T(8,128)(2,1)S(1)} all-gather(bf16[1,64,32]{1,2,0:T(8,128)(2,1)S(1)} %fusion.2), channel_id=1, replica_groups=mesh['bank'=4,'zero'=32] {'zero'}, dimensions={0}, use_global_device_ids=true | all-gather | bytes 135168 | tf_op jit(solution)/shard_map/all_gather | solution.py:22
  179.1 0.1 copy.13
  179.2 0.3 reshape.148
  179.5 21.2 %all_gather.7 = bf16[2048,128]{0,1:T(8,128)(2,1)} all-gather(bf16[2048,32]{0,1:T(8,128)(2,1)S(1)} %reshape.148), channel_id=1, replica_groups=mesh['bank'=4,'zero'=32] {'bank'}, dimensions={1}, use_global_device_ids=true | all-gather | bytes 655360 | tf_op jit(solution)/shard_map/all_gather | solution.py:23
  200.7 2.0 copy.14
  202.8 2.6 %multiply_reduce_fusion = f32[768]{0:T(1024)S(1)} fusion(bf16[32,64,768]{2,1,0:T(8,128)(2,1)} %copy-done), kind=kLoop, calls=%fused_computation.4 | loop fusion | flops 4717824 | bytes 3148800 | tf_op jit(solution)/shard_map/reduce_sum | solution.py:14
  205.4 0.6 sqrt.39
  206.0 2.7 %convert_element_type.89 = f32[32,64,768]{2,1,0:T(8,128)S(1)} convert(bf16[32,64,768]{2,1,0:T(8,128)(2,1)} %copy-done) | non-fusion elementwise | flops 1572864 | bytes 9437184 | tf_op jit(solution)/shard_map/convert_element_type | solution.py:13
  208.6 2.3 %fusion = bf16[1,2048,768]{2,1,0:T(8,128)(2,1)} fusion(f32[768]{0:T(1024)S(1)} %sqrt.37, f32[1,2048,768]{2,1,0:T(8,128)S(1)} %bitcast.14), kind=kLoop, calls=%fused_computation.1 | loop fusion | flops 3145728 | bytes 9440256 | tf_op jit(solution)/shard_map/convert_element_type | solution.py:15
  210.9 0.0 all-to-all-done
  210.9 0.7 multiply_reduce_fusion.1
  211.7 0.6 sqrt.38
  212.2 0.8 convert_element_type.88
  213.0 2.3 %fusion.1 = bf16[1,2048,768]{2,1,0:T(8,128)(2,1)} fusion(f32[768]{0:T(1024)S(1)} %sqrt.36, f32[1,2048,768]{2,1,0:T(8,128)S(1)} %bitcast.15), kind=kLoop, calls=%fused_computation.3 | loop fusion | flops 3145728 | bytes 9440256 | tf_op jit(solution)/shard_map/convert_element_type | solution.py:15
  (3 shorter events, 0.0 us)
Async XLA Ops:
  7.0 51.7 %all-to-all-start.1 = ((bf16[32,64,768]{2,1,0:T(8,128)(2,1)}), bf16[32,64,768]{2,1,0:T(8,128)(2,1)S(1)}, u32[]{:S(2)}, u32[]{:S(2)}) async-start(bf16[32,64,768]{2,1,0:T(8,128)(2,1)} %add_convert_fusion), calls=%async_computation.1 | async-start | bytes 6291456 | tf_op jit(solution)/shard_map/all_to_all | solution.py:9
  24.8 44.8 %copy-start.1 = (f32[64,32]{0,1:T(8,128)S(1)}, f32[64,32]{0,1:T(8,128)}, u32[]{:S(2)}) copy-start(f32[64,32]{0,1:T(8,128)} %param.10) | copy-start | bytes 24580
  24.8 44.8 %copy-start.2 = (f32[64]{0:T(128)S(1)}, f32[64]{0:T(128)}, u32[]{:S(2)}) copy-start(f32[64]{0:T(128)} %param.11) | copy-start | bytes 772
  58.8 1.7 copy-start
  60.5 150.5 %all-to-all-start = ((bf16[32,64,768]{2,1,0:T(8,128)(2,1)}), bf16[32,64,768]{2,1,0:T(8,128)(2,1)S(1)}, u32[]{:S(2)}, u32[]{:S(2)}) async-start(bf16[32,64,768]{2,1,0:T(8,128)(2,1)} %add_convert_fusion.1), calls=%async_computation | async-start | bytes 6291456 | tf_op jit(solution)/shard_map/all_to_all | solution.py:9
where the time goes:
time: 216 us; the launch traced here: 215 us
  blocking collectives  131 us (61%)
  waiting for transfers between devices  34 us (16%)
  other arithmetic  24.2 us (11%)
  starting transfers between devices  20.5 us (9%)
  local copies, waits for them, and re-layouts  5.28 us (2%)
    all_gather x1, blocking collectives, body(): serve_router = lax.all_gather(part_router, 'zero', axis=0, tiled=True)  109 us
    all_to_all x2, waiting for transfers between devices, regrouped(): lax.all_to_all(latest, 'zero', split_axis=0, concat_axis=1, tiled=True)  34 us
    all_gather x1, blocking collectives, body(): serve_router = lax.all_gather(serve_router, 'bank', axis=1, tiled=True)  21.2 us
    all_to_all x2, starting transfers between devices, regrouped(): lax.all_to_all(latest, 'zero', split_axis=0, concat_axis=1, tiled=True)  20.5 us
    convert_element_type x2, other arithmetic, regrouped(): latest = (train + other.astype(jnp.float32)).astype(jnp.bfloat16)  12.8 us
    convert_element_type x2, other arithmetic, normalised(): return ((wide / scale[:, None, :]).astype(jnp.bfloat16), scale)  4.52 us
  transfers between devices with their start and end apart: 2, of which 1 were waited for; matrix products, arithmetic and copies ran while one was open for 8% of the time, Pallas kernels for 0%

commit v1 on v0

--- a/solution.py
+++ b/solution.py
@@ -20,7 +20,7 @@
     up = regrouped(train_up, other_up)
     part_router = (router_weight * router_gain[:, None]).astype(jnp.bfloat16)
     serve_router = lax.all_gather(part_router, "zero", axis=0, tiled=True)
-    serve_router = lax.all_gather(serve_router, "bank", axis=1, tiled=True)
+    serve_router = jnp.concatenate(lax.all_gather(serve_router, "bank"), axis=1)
     ready_gate, scale_gate = normalised(gate)
     ready_up, scale_up = normalised(up)
     return (ready_gate, ready_up, scale_gate, scale_up, serve_router)

time: 216 us -> 220 us (1.019)
  local copies, waits for them, and re-layouts: 5.28 us -> 9.61 us
    all_gather x0 -> x1, local copies, waits for them, and re-layouts: none -> 2.22 us  [body(): serve_router = jnp.concatenate(lax.all_gather(serve_router, 'bank'), axis=1)]
  transfers between devices with their start and end apart: 2 -> 2, of which waited for: 1 -> 1; matrix products, arithmetic and copies ran while one was open for 8% -> 10% of each run, Pallas kernels for 0% -> 0%
where the time goes in v1:
time: 220 us
  blocking collectives  131 us (60%)
  waiting for transfers between devices  34 us (15%)
  other arithmetic  24.2 us (11%)
  starting transfers between devices  20.5 us (9%)
  local copies, waits for them, and re-layouts  9.61 us (4%)
    all_gather x1, blocking collectives, body(): serve_router = lax.all_gather(part_router, 'zero', axis=0, tiled=True)  109 us
    all_to_all x2, waiting for transfers between devices, regrouped(): lax.all_to_all(latest, 'zero', split_axis=0, concat_axis=1, tiled=True)  34 us
    all_gather x1, blocking collectives, body(): serve_router = jnp.concatenate(lax.all_gather(serve_router, 'bank'), axis=1)  21.2 us
    all_to_all x2, starting transfers between devices, regrouped(): lax.all_to_all(latest, 'zero', split_axis=0, concat_axis=1, tiled=True)  20.5 us
    convert_element_type x2, other arithmetic, regrouped(): latest = (train + other.astype(jnp.float32)).astype(jnp.bfloat16)  12.8 us
    convert_element_type x2, other arithmetic, normalised(): return ((wide / scale[:, None, :]).astype(jnp.bfloat16), scale)  4.52 us
  transfers between devices with their start and end apart: 2, of which 1 were waited for; matrix products, arithmetic and copies ran while one was open for 10% of the time, Pallas kernels for 0%

profile of v1, /device:TPU:1, one launch (start us, length us, event | category | flops | bytes accessed | tf_op | source)
XLA Modules:
  0.0 219.6 jit_solution(15445600055573571469)
XLA Ops:
  0.6 6.4 %add_convert_fusion = bf16[32,64,768]{2,1,0:T(8,128)(2,1)} fusion(f32[32,64,768]{2,1,0:T(8,128)} %param.8, bf16[32,64,768]{2,1,0:T(8,128)(2,1)} %param.9), kind=kLoop, calls=%fused_computation.5 | loop fusion | flops 4718592 | bytes 12582912 | tf_op jit(solution)/shard_map/convert_element_type | solution.py:8
  7.0 11.3 %all-to-all-start.1 = ((bf16[32,64,768]{2,1,0:T(8,128)(2,1)}), bf16[32,64,768]{2,1,0:T(8,128)(2,1)S(1)}, u32[]{:S(2)}, u32[]{:S(2)}) async-start(bf16[32,64,768]{2,1,0:T(8,128)(2,1)} %add_convert_fusion), calls=%async_computation.1 | async-start | bytes 6291456 | tf_op jit(solution)/shard_map/all_to_all | solution.py:9
  18.4 6.4 %add_convert_fusion.1 = bf16[32,64,768]{2,1,0:T(8,128)(2,1)} fusion(f32[32,64,768]{2,1,0:T(8,128)} %param.6, bf16[32,64,768]{2,1,0:T(8,128)(2,1)} %param.7), kind=kLoop, calls=%fused_computation.7 | loop fusion | flops 4718592 | bytes 12582912 | tf_op jit(solution)/shard_map/convert_element_type | solution.py:8
  24.8 0.0 copy-start.1
  24.8 0.0 copy-start.2
  24.8 34.0 %all-to-all-done.1 = bf16[32,64,768]{2,1,0:T(8,128)(2,1)S(1)} async-done(((bf16[32,64,768]{2,1,0:T(8,128)(2,1)}), bf16[32,64,768]{2,1,0:T(8,128)(2,1)S(1)}, u32[]{:S(2)}, u32[]{:S(2)}) %all-to-all-start.1) | async-done | bytes 3145760 | tf_op jit(solution)/shard_map/all_to_all | solution.py:9
  58.8 0.0 copy-start
  58.8 1.7 copy-done
  60.5 9.2 %all-to-all-start = ((bf16[32,64,768]{2,1,0:T(8,128)(2,1)}), bf16[32,64,768]{2,1,0:T(8,128)(2,1)S(1)}, u32[]{:S(2)}, u32[]{:S(2)}) async-start(bf16[32,64,768]{2,1,0:T(8,128)(2,1)} %add_convert_fusion.1), calls=%async_computation | async-start | bytes 6291456 | tf_op jit(solution)/shard_map/all_to_all | solution.py:9
  69.6 0.0 copy-done.1
  69.6 0.0 copy-done.2
  69.7 109.4 %all-gather.1 = bf16[32,64,32]{1,2,0:T(8,128)(2,1)S(1)} all-gather(bf16[1,64,32]{1,2,0:T(8,128)(2,1)S(1)} %fusion.2), channel_id=1, replica_groups=mesh['bank'=4,'zero'=32] {'zero'}, dimensions={0}, use_global_device_ids=true | all-gather | bytes 135168 | tf_op jit(solution)/shard_map/all_gather | solution.py:22
  179.1 0.1 copy.14
  179.2 0.3 reshape.157
  179.5 21.2 %all-gather = bf16[8192,32]{0,1:T(8,128)(2,1)} all-gather(bf16[2048,32]{0,1:T(8,128)(2,1)S(1)} %reshape.157), channel_id=2, replica_groups=mesh['bank'=4,'zero'=32] {'bank'}, dimensions={0}, use_global_device_ids=true | all-gather | bytes 655360 | tf_op jit(solution)/shard_map/all_gather | solution.py:23
  200.7 2.2 %reshape.155 = bf16[4,2048,32]{1,0,2:T(4,128)(2,1)} reshape(bf16[8192,32]{0,1:T(8,128)(2,1)} %all-gather) | data formatting | bytes 1048576 | tf_op jit(solution)/shard_map/all_gather | solution.py:23
  202.9 2.1 copy.15
  205.0 2.0 copy.16
  207.1 2.6 %multiply_reduce_fusion = f32[768]{0:T(1024)S(1)} fusion(bf16[32,64,768]{2,1,0:T(8,128)(2,1)} %copy-done), kind=kLoop, calls=%fused_computation.4 | loop fusion | flops 4717824 | bytes 3148800 | tf_op jit(solution)/shard_map/reduce_sum | solution.py:14
  209.7 0.6 sqrt.39
  210.3 2.7 %convert_element_type.89 = f32[32,64,768]{2,1,0:T(8,128)S(1)} convert(bf16[32,64,768]{2,1,0:T(8,128)(2,1)} %copy-done) | non-fusion elementwise | flops 1572864 | bytes 9437184 | tf_op jit(solution)/shard_map/convert_element_type | solution.py:13
  213.0 2.3 %fusion = bf16[1,2048,768]{2,1,0:T(8,128)(2,1)} fusion(f32[768]{0:T(1024)S(1)} %sqrt.37, f32[1,2048,768]{2,1,0:T(8,128)S(1)} %bitcast.18), kind=kLoop, calls=%fused_computation.1 | loop fusion | flops 3145728 | bytes 9440256 | tf_op jit(solution)/shard_map/convert_element_type | solution.py:15
  215.2 0.0 all-to-all-done
  215.2 0.7 multiply_reduce_fusion.1
  216.0 0.6 sqrt.38
  216.6 0.8 convert_element_type.88
  217.4 2.3 %fusion.1 = bf16[1,2048,768]{2,1,0:T(8,128)(2,1)} fusion(f32[768]{0:T(1024)S(1)} %sqrt.36, f32[1,2048,768]{2,1,0:T(8,128)S(1)} %bitcast.19), kind=kLoop, calls=%fused_computation.3 | loop fusion | flops 3145728 | bytes 9440256 | tf_op jit(solution)/shard_map/convert_element_type | solution.py:15
  (3 shorter events, 0.0 us)
Async XLA Ops:
  7.0 51.7 %all-to-all-start.1 = ((bf16[32,64,768]{2,1,0:T(8,128)(2,1)}), bf16[32,64,768]{2,1,0:T(8,128)(2,1)S(1)}, u32[]{:S(2)}, u32[]{:S(2)}) async-start(bf16[32,64,768]{2,1,0:T(8,128)(2,1)} %add_convert_fusion), calls=%async_computation.1 | async-start | bytes 6291456 | tf_op jit(solution)/shard_map/all_to_all | solution.py:9
  24.8 44.8 %copy-start.1 = (f32[64,32]{0,1:T(8,128)S(1)}, f32[64,32]{0,1:T(8,128)}, u32[]{:S(2)}) copy-start(f32[64,32]{0,1:T(8,128)} %param.10) | copy-start | bytes 24580
  24.8 44.8 %copy-start.2 = (f32[64]{0:T(128)S(1)}, f32[64]{0:T(128)}, u32[]{:S(2)}) copy-start(f32[64]{0:T(128)} %param.11) | copy-start | bytes 772
  58.8 1.7 copy-start
  60.5 154.8 %all-to-all-start = ((bf16[32,64,768]{2,1,0:T(8,128)(2,1)}), bf16[32,64,768]{2,1,0:T(8,128)(2,1)S(1)}, u32[]{:S(2)}, u32[]{:S(2)}) async-start(bf16[32,64,768]{2,1,0:T(8,128)(2,1)} %add_convert_fusion.1), calls=%async_computation | async-start | bytes 6291456 | tf_op jit(solution)/shard_map/all_to_all | solution.py:9

commit v2 on v0

--- a/solution.py
+++ b/solution.py
@@ -19,7 +19,9 @@
     gate = regrouped(train_gate, other_gate)
     up = regrouped(train_up, other_up)
     part_router = (router_weight * router_gain[:, None]).astype(jnp.bfloat16)
-    serve_router = lax.all_gather(part_router, "zero", axis=0, tiled=True)
+    serve_router = jnp.concatenate(
+        lax.all_to_all(jnp.stack([part_router] * lax.axis_size("zero")), "zero", 0, 0), axis=0
+    )
     serve_router = lax.all_gather(serve_router, "bank", axis=1, tiled=True)
     ready_gate, scale_gate = normalised(gate)
     ready_up, scale_up = normalised(up)

time: 216 us -> 142 us (0.66)
  the two profiles are of different devices: /device:TPU:1 before, /device:TPU:19 now
where the time goes in v2:
time: 142 us; the launch traced here: 141 us
  blocking collectives  44.2 us (31%)
  waiting for transfers between devices  38.2 us (27%)
  starting transfers between devices  25.5 us (18%)
  other arithmetic  24.9 us (18%)
  local copies, waits for them, and re-layouts  8.03 us (6%)
    all_gather x1, blocking collectives, body(): serve_router = lax.all_gather(serve_router, 'bank', axis=1, tiled=True)  44.2 us
    all_to_all x2, waiting for transfers between devices, regrouped(): lax.all_to_all(latest, 'zero', split_axis=0, concat_axis=1, tiled=True)  38.2 us
    all_to_all x2, starting transfers between devices, regrouped(): lax.all_to_all(latest, 'zero', split_axis=0, concat_axis=1, tiled=True)  15.2 us
    convert_element_type x2, other arithmetic, regrouped(): latest = (train + other.astype(jnp.float32)).astype(jnp.bfloat16)  12.8 us
    all_to_all x1, starting transfers between devices, body(): lax.all_to_all(jnp.stack([part_router] * lax.axis_size('zero')), 'zero',...  10.3 us
    unnamed x6, local copies, waits for them, and re-layouts  4.81 us
    convert_element_type x2, other arithmetic, normalised(): return ((wide / scale[:, None, :]).astype(jnp.bfloat16), scale)  4.52 us
    convert_element_type x2, other arithmetic, normalised(): wide = pieces.astype(jnp.float32)  3.44 us
  transfers between devices with their start and end apart: 3, of which 1 were waited for; matrix products, arithmetic and copies ran while one was open for 18% of the time, Pallas kernels for 0%

profile of v2, /device:TPU:19, one launch (start us, length us, event | category | flops | bytes accessed | tf_op | source)
XLA Modules:
  0.0 141.4 jit_solution(12718003715768044233)
XLA Ops:
  0.6 0.7 multiply_convert_fusion
  1.4 0.8 reshape.153
  2.2 10.3 %all-to-all-start.2 = ((bf16[32,2,1024]{2,1,0:T(2,128)(2,1)}), bf16[32,2,1024]{2,1,0:T(2,128)(2,1)S(1)}, u32[]{:S(2)}, u32[]{:S(2)}) async-start(bf16[32,2,1024]{2,1,0:T(2,128)(2,1)} %reshape.153), calls=%async_computation.2 | async-start | bytes 262144 | tf_op jit(solution)/shard_map/all_to_all | solution.py:23
  12.6 6.4 %add_convert_fusion = bf16[32,64,768]{2,1,0:T(8,128)(2,1)} fusion(f32[32,64,768]{2,1,0:T(8,128)} %param.8, bf16[32,64,768]{2,1,0:T(8,128)(2,1)} %param.9), kind=kLoop, calls=%fused_computation.5 | loop fusion | flops 4718592 | bytes 12582912 | tf_op jit(solution)/shard_map/convert_element_type | solution.py:8
  19.0 0.0 all-to-all-done.2
  19.0 9.2 %all-to-all-start.1 = ((bf16[32,64,768]{2,1,0:T(8,128)(2,1)}), bf16[32,64,768]{2,1,0:T(8,128)(2,1)S(1)}, u32[]{:S(2)}, u32[]{:S(2)}) async-start(bf16[32,64,768]{2,1,0:T(8,128)(2,1)} %add_convert_fusion), calls=%async_computation.1 | async-start | bytes 6291456 | tf_op jit(solution)/shard_map/all_to_all | solution.py:9
  28.2 6.4 %add_convert_fusion.1 = bf16[32,64,768]{2,1,0:T(8,128)(2,1)} fusion(f32[32,64,768]{2,1,0:T(8,128)} %param.6, bf16[32,64,768]{2,1,0:T(8,128)(2,1)} %param.7), kind=kLoop, calls=%fused_computation.7 | loop fusion | flops 4718592 | bytes 12582912 | tf_op jit(solution)/shard_map/convert_element_type | solution.py:8
  34.6 38.2 %all-to-all-done.1 = bf16[32,64,768]{2,1,0:T(8,128)(2,1)S(1)} async-done(((bf16[32,64,768]{2,1,0:T(8,128)(2,1)}), bf16[32,64,768]{2,1,0:T(8,128)(2,1)S(1)}, u32[]{:S(2)}, u32[]{:S(2)}) %all-to-all-start.1) | async-done | bytes 3145760 | tf_op jit(solution)/shard_map/all_to_all | solution.py:9
  72.8 0.0 copy-start
  72.8 1.7 %copy-done = bf16[32,64,768]{2,1,0:T(8,128)(2,1)} copy-done((bf16[32,64,768]{2,1,0:T(8,128)(2,1)}, bf16[32,64,768]{2,1,0:T(8,128)(2,1)S(1)}, u32[]{:S(2)}) %copy-start) | copy-done | bytes 3145752
  74.5 5.9 %all-to-all-start = ((bf16[32,64,768]{2,1,0:T(8,128)(2,1)}), bf16[32,64,768]{2,1,0:T(8,128)(2,1)S(1)}, u32[]{:S(2)}, u32[]{:S(2)}) async-start(bf16[32,64,768]{2,1,0:T(8,128)(2,1)} %add_convert_fusion.1), calls=%async_computation | async-start | bytes 6291456 | tf_op jit(solution)/shard_map/all_to_all | solution.py:9
  80.4 0.2 reshape.154
  80.6 0.8 copy.13
  81.4 1.2 reshape.150
  82.7 44.2 %all_gather.3 = bf16[2048,128]{0,1:T(8,128)(2,1)} all-gather(bf16[2048,32]{0,1:T(8,128)(2,1)S(1)} %reshape.150), channel_id=1, replica_groups=mesh['bank'=4,'zero'=32] {'bank'}, dimensions={1}, use_global_device_ids=true | all-gather | bytes 655360 | tf_op jit(solution)/shard_map/all_gather | solution.py:25
  126.9 2.0 %copy.14 = bf16[2048,128]{1,0:T(8,128)(2,1)} copy(bf16[2048,128]{0,1:T(8,128)(2,1)} %all_gather.3) | data formatting | bytes 1048576
  128.9 2.6 %multiply_reduce_fusion = f32[768]{0:T(1024)S(1)} fusion(bf16[32,64,768]{2,1,0:T(8,128)(2,1)} %copy-done), kind=kLoop, calls=%fused_computation.4 | loop fusion | flops 4717824 | bytes 3148800 | tf_op jit(solution)/shard_map/reduce_sum | solution.py:14
  131.5 0.6 sqrt.39
  132.1 2.7 %convert_element_type.89 = f32[32,64,768]{2,1,0:T(8,128)S(1)} convert(bf16[32,64,768]{2,1,0:T(8,128)(2,1)} %copy-done) | non-fusion elementwise | flops 1572864 | bytes 9437184 | tf_op jit(solution)/shard_map/convert_element_type | solution.py:13
  134.8 2.3 %fusion = bf16[1,2048,768]{2,1,0:T(8,128)(2,1)} fusion(f32[768]{0:T(1024)S(1)} %sqrt.37, f32[1,2048,768]{2,1,0:T(8,128)S(1)} %bitcast.15), kind=kLoop, calls=%fused_computation.1 | loop fusion | flops 3145728 | bytes 9440256 | tf_op jit(solution)/shard_map/convert_element_type | solution.py:15
  137.1 0.0 all-to-all-done
  137.1 0.7 multiply_reduce_fusion.1
  137.8 0.6 sqrt.38
  138.4 0.8 convert_element_type.88
  139.2 2.3 %fusion.1 = bf16[1,2048,768]{2,1,0:T(8,128)(2,1)} fusion(f32[768]{0:T(1024)S(1)} %sqrt.36, f32[1,2048,768]{2,1,0:T(8,128)S(1)} %bitcast.16), kind=kLoop, calls=%fused_computation.3 | loop fusion | flops 3145728 | bytes 9440256 | tf_op jit(solution)/shard_map/convert_element_type | solution.py:15
  (3 shorter events, 0.1 us)
Async XLA Ops:
  2.2 16.7 %all-to-all-start.2 = ((bf16[32,2,1024]{2,1,0:T(2,128)(2,1)}), bf16[32,2,1024]{2,1,0:T(2,128)(2,1)S(1)}, u32[]{:S(2)}, u32[]{:S(2)}) async-start(bf16[32,2,1024]{2,1,0:T(2,128)(2,1)} %reshape.153), calls=%async_computation.2 | async-start | bytes 262144 | tf_op jit(solution)/shard_map/all_to_all | solution.py:23
  19.0 53.8 %all-to-all-start.1 = ((bf16[32,64,768]{2,1,0:T(8,128)(2,1)}), bf16[32,64,768]{2,1,0:T(8,128)(2,1)S(1)}, u32[]{:S(2)}, u32[]{:S(2)}) async-start(bf16[32,64,768]{2,1,0:T(8,128)(2,1)} %add_convert_fusion), calls=%async_computation.1 | async-start | bytes 6291456 | tf_op jit(solution)/shard_map/all_to_all | solution.py:9
  72.8 1.7 %copy-start = (bf16[32,64,768]{2,1,0:T(8,128)(2,1)}, bf16[32,64,768]{2,1,0:T(8,128)(2,1)S(1)}, u32[]{:S(2)}) copy-start(bf16[32,64,768]{2,1,0:T(8,128)(2,1)S(1)} %all-to-all-done.1) | copy-start | bytes 9437188
  74.5 62.6 %all-to-all-start = ((bf16[32,64,768]{2,1,0:T(8,128)(2,1)}), bf16[32,64,768]{2,1,0:T(8,128)(2,1)S(1)}, u32[]{:S(2)}, u32[]{:S(2)}) async-start(bf16[32,64,768]{2,1,0:T(8,128)(2,1)} %add_convert_fusion.1), calls=%async_computation | async-start | bytes 6291456 | tf_op jit(solution)/shard_map/all_to_all | solution.py:9
